TPU v7x, 32 devices: a whole 2x2x4 slice. The times are simulated.
32 devices in a mesh: member: 8 (over z, y), region: 4 (over x, core).
Axes of the slice: x: 2, y: 2, z: 4, core: 2. Of those that a mesh axis runs over, the one named last changes fastest.
Arguments:
- ensemble: bfloat16 [512, 32768], P(('member', 'region')), may hold values from -12 to 12
- obs_offset: int32 [4, 8, 16], P('region', 'member'), may hold values from 0 to 1023
- observed: float32 [4, 8, 16], P('region', 'member'), may hold values from -12 to 12
- obs_var: float32 [4, 8, 16], P('region', 'member'), may hold values from 0.2 to 2
Outputs:
- analysis: bfloat16 [512, 32768], P(('member', 'region'))
Inputs may be any that keep to these rules, and one draw needn't show every extreme that they name: obs_offset indexes a link within the block of 1024 links; two detectors may watch the same link.
All inputs are finite; a program needn't handle non-finite values.
Results may differ from a plain program's by a relative error of at most 0.0019.
Values may be sent and summed in bfloat16 or wider, within the bound.
A program may use at most 128 MiB of HBM per device.

v0:
```python
import jax
import jax.numpy as jnp
from jax import lax
from jax.sharding import PartitionSpec as P


def observation_terms(picked, values, variance, ensemble_size):
    center = jnp.mean(picked, axis=1, keepdims=True)
    anomaly = picked - center
    innovation = values - center[:, 0]
    numer = jnp.sum(innovation * innovation)
    denom = jnp.sum(jnp.sum(anomaly * anomaly, axis=1) / (ensemble_size - 1.0) + variance)
    weight = 1.0 / ((ensemble_size - 1.0) * variance)
    return (anomaly, innovation, weight, numer, denom)


def weighted_products(anomaly, innovation, weight):
    weighted = anomaly * weight[:, None]
    products = jnp.dot(weighted.T, anomaly, precision=lax.Precision.HIGHEST)
    column = jnp.dot(innovation * weight, anomaly, precision=lax.Precision.HIGHEST)
    return (products, column)


def mixing_matrix(products, column, lift, diag_coef, col_coef, mat_coef):
    identity = jnp.eye(products.shape[0], dtype=jnp.float32)
    system = identity + lift * products
    factor = jnp.linalg.cholesky(system)
    right_side = jnp.concatenate([products, column[:, None]], axis=1)
    solved = jax.scipy.linalg.cho_solve((factor, True), right_side)
    return diag_coef * identity + col_coef * solved[:, -1][None, :] - mat_coef * solved[:, :-1]


def local(ensemble, obs_offset, observed, obs_var):
    members = lax.axis_size("member")
    regions = lax.axis_size("region")
    own_count = ensemble.shape[0]
    ensemble_size = own_count * members * regions
    link_count = ensemble.shape[1] // (members * regions)
    shifted = lax.all_to_all(
        lax.all_to_all(ensemble, "region", split_axis=1, concat_axis=0, tiled=True),
        "member",
        split_axis=1,
        concat_axis=0,
        tiled=True,
    )
    values = observed.reshape(-1)
    variance = obs_var.reshape(-1)
    region_offsets = lax.all_gather(obs_offset, "member", axis=1, tiled=True)
    every_offset = lax.all_gather(region_offsets, "region", axis=0, tiled=True)
    region_block = lax.broadcasted_iota(jnp.int32, every_offset.shape, 0)
    member_block = lax.broadcasted_iota(jnp.int32, every_offset.shape, 1)
    link_index = ((region_block * members + member_block) * link_count + every_offset).reshape(-1)
    own_rows = jnp.take(ensemble, link_index, axis=1).reshape(own_count, regions, -1)
    local_rows = lax.all_to_all(own_rows, "region", split_axis=1, concat_axis=0, tiled=True)
    local_rows = local_rows.reshape(own_count * regions, -1)
    obs_rows = lax.all_gather(local_rows, "member", axis=0, tiled=True)
    region_values, region_variance = (
        lax.all_gather(values, "member", axis=0, tiled=True),
        lax.all_gather(variance, "member", axis=0, tiled=True),
    )
    picked = obs_rows.T.astype(jnp.float32)
    anomaly, innovation, weight, numer, denom = observation_terms(
        picked, region_values, region_variance, ensemble_size
    )
    numer, denom = lax.psum((numer, denom), "region")
    inflation = jnp.sqrt(numer / denom)
    products, column = weighted_products(inflation * anomaly, innovation, weight)
    products, column = lax.psum((products, column), "region")
    mixing = mixing_matrix(products, column, 1.0, inflation, inflation, 0.5 * inflation)
    state_values = shifted.astype(jnp.float32)
    center = jnp.mean(state_values, axis=0, keepdims=True)
    updated = (
        center + jnp.dot(mixing, state_values - center, precision=lax.Precision.HIGHEST)
    ).astype(jnp.bfloat16)
    return lax.all_to_all(
        lax.all_to_all(updated, "member", split_axis=0, concat_axis=1, tiled=True),
        "region",
        split_axis=0,
        concat_axis=1,
        tiled=True,
    )


def solution(mesh):
    return jax.shard_map(
        local,
        mesh=mesh,
        in_specs=(
            P(("member", "region"), None),
            P("region", "member", None),
            P("region", "member", None),
            P("region", "member", None),
        ),
        out_specs=P(("member", "region"), None),
        check_vma=False,
    )
```

profile of v0, /device:TPU:0, one launch (start us, length us, event | category | flops | bytes accessed | tf_op | source)
XLA Modules:
  0.0 394.1 jit_solution(4288350001859366908)
XLA Ops:
  6.5 22.5 %all_gather.16 = s32[1,8,16]{2,0,1:T(1,128)S(1)} all-gather(s32[1,1,16]{2,0,1:T(1,128)} %bitcast.112), channel_id=1, replica_groups=mesh['member'=8,'region'=4] {'member'}, dimensions={1}, use_global_device_ids=true | all-gather | bytes 576 | tf_op jit(solution)/shard_map/all_gather | solution.py:48
  29.0 5.2 %all_gather.17 = s32[4,8,16]{2,1,0:T(8,128)S(1)} all-gather(s32[1,8,16]{2,1,0:T(8,128)S(1)} %bitcast.109), channel_id=1, replica_groups=mesh['member'=8,'region'=4] {'region'}, dimensions={0}, use_global_device_ids=true | all-gather | bytes 2560 | tf_op jit(solution)/shard_map/all_gather | solution.py:49
  34.5 7.1 %copy.51 = bf16[16,32768]{0,1:T(8,128)(2,1)} copy(bf16[16,32768]{1,0:T(8,128)(2,1)} %param.4) | data formatting | bytes 2097152 | tf_op args[0]
  41.5 5.6 %gather_fusion = bf16[512,16]{1,0:T(8,128)(2,1)S(1)} fusion(bf16[16,32768]{0,1:T(8,128)(2,1)} %copy.51, s32[1024]{0:T(1024)S(1)} %pad_clamp_fusion), kind=kCustom, calls=%fused_computation | custom fusion | bytes 34816 | tf_op jit(solution)/shard_map/jit(_take)/gather | solution.py:53
  52.8 17.1 %all-reduce.3 = (f32[128]{0:T(128)S(1)}, f32[128]{0:T(128)S(1)}) all-reduce(f32[128]{0:T(128)S(1)} %bitcast_dynamic-update-slice_fusion.1, f32[128]{0:T(128)S(1)} %bitcast_dynamic-update-slice_fusion.2), channel_id=3, replica_groups=mesh['member'=8,'region'=4] {'member'}, use_global_device_ids=true, to_apply=%add.2 | all-reduce | flops 256 | bytes 2048 | tf_op jit(solution)/shard_map/all_gather | solution.py:59
  69.9 30.5 %all_gather.18 = bf16[512,128]{1,0:T(8,128)(2,1)S(1)} all-gather(bf16[64,128]{1,0:T(8,128)(2,1)S(1)} %bitcast.108), channel_id=1, replica_groups=mesh['member'=8,'region'=4] {'member'}, dimensions={0}, use_global_device_ids=true | all-gather | bytes 147456 | tf_op jit(solution)/shard_map/all_gather | solution.py:56
  101.8 6.3 %all-reduce.4 = (f32[]{:T(128)}, f32[]{:T(128)}) all-reduce(f32[]{:T(128)} %get-tuple-element.54, f32[]{:T(128)} %get-tuple-element.51), channel_id=1, replica_groups=mesh['member'=8,'region'=4] {'region'}, use_global_device_ids=true, to_apply=%region_3.4 | all-reduce | flops 2 | bytes 16 | tf_op jit(solution)/shard_map/psum | solution.py:65
  112.5 4.2 %all-to-all-start = ((bf16[16,4,8192]{2,0,1:T(8,128)(2,1)}), bf16[16,4,8192]{2,0,1:T(8,128)(2,1)}, u32[]{:S(2)}, u32[]{:S(2)}) async-start(bf16[16,4,8192]{2,0,1:T(8,128)(2,1)} %bitcast.95), calls=%async_computation | async-start | bytes 2097152 | tf_op jit(solution)/shard_map/all_to_all | solution.py:40
  117.1 22.4 %psum.31 = f32[512,1]{0,1:T(1,128)S(1)} all-reduce(f32[512,1]{0,1:T(1,128)S(1)} %convolution_bitcast_fusion), channel_id=1, replica_groups=mesh['member'=8,'region'=4] {'region'}, use_global_device_ids=true, to_apply=%region_16.17 | all-reduce | flops 512 | bytes 4096 | tf_op jit(solution)/shard_map/psum | solution.py:68
  139.5 14.7 %all-reduce.7.cloned.1.call-done = f32[512,512]{0,1:T(8,128)} async-done(((f32[512,512]{0,1:T(8,128)}), f32[512,512]{0,1:T(8,128)}) %all-reduce.7.cloned.1.call-update) | async-done | bytes 1048592 | tf_op jit(solution)/shard_map/psum | solution.py:68
  158.7 11.7 %cholesky.103 = f32[128,128]{1,0:T(8,128)S(1)} custom-call(f32[128,128]{1,0:T(8,128)S(1)} %cholesky.263), custom_call_target="Cholesky" | custom-call | tf_op jit(solution)/shard_map/jit(cholesky)/cholesky | solution.py:27
  170.4 9.8 %custom-call.34 = f32[1,128,128]{1,2,0:T(8,128)S(1)} custom-call(f32[1,128,128]{2,1,0:T(8,128)S(1)} %get-tuple-element.50), custom_call_target="InvertDiagBlocksLowerTriangular" | custom-call | tf_op jit(solution)/shard_map/jit(cholesky)/cholesky | solution.py:27
  180.9 11.7 %cholesky.215 = f32[128,128]{1,0:T(8,128)S(1)} custom-call(f32[128,128]{1,0:T(8,128)S(1)} %cholesky.267), custom_call_target="Cholesky" | custom-call | tf_op jit(solution)/shard_map/jit(cholesky)/cholesky | solution.py:27
  193.0 10.0 %custom-call.35 = f32[1,128,128]{1,2,0:T(8,128)S(1)} custom-call(f32[1,128,128]{2,1,0:T(8,128)S(1)} %get-tuple-element.48), custom_call_target="InvertDiagBlocksLowerTriangular" | custom-call | tf_op jit(solution)/shard_map/jit(cholesky)/cholesky | solution.py:27
  205.0 11.7 %cholesky.236 = f32[128,128]{1,0:T(8,128)S(1)} custom-call(f32[128,128]{1,0:T(8,128)S(1)} %cholesky.272), custom_call_target="Cholesky" | custom-call | tf_op jit(solution)/shard_map/jit(cholesky)/cholesky | solution.py:27
  216.8 9.8 %custom-call.36 = f32[1,128,128]{1,2,0:T(8,128)S(1)} custom-call(f32[1,128,128]{2,1,0:T(8,128)S(1)} %get-tuple-element.46), custom_call_target="InvertDiagBlocksLowerTriangular" | custom-call | tf_op jit(solution)/shard_map/jit(cholesky)/cholesky | solution.py:27
  228.3 12.1 %cholesky.253 = f32[128,128]{1,0:T(8,128)S(1)} custom-call(f32[128,128]{1,0:T(8,128)S(1)} %convolution_subtract_fusion.8), custom_call_target="Cholesky" | custom-call | tf_op jit(solution)/shard_map/jit(cholesky)/cholesky | solution.py:27
  245.2 11.0 %while.1 = (s32[]{:T(128)}, f32[512,512]{0,1:T(8,128)S(1)}, s32[4,2]{0,1:T(2,128)S(1)}, f32[4,128,128]{2,1,0:T(8,128)}, s32[]{:T(128)}) while((s32[]{:T(128)}, f32[512,512]{0,1:T(8,128)S(1)}, s32[4,2]{0,1:T(2,128)S(1)}, f32[4,128,128]{2,1,0:T(8,128)}, s32[]{:T(128)}) %tuple.30), condition=%wide.while_cond, body=%wide.while_body.sunk | while | flops 2 | bytes 393829 | solution.py:29
  256.2 40.1 %custom-call.37 = f32[4,128,128]{1,2,0:T(8,128)S(1)} custom-call(f32[4,128,128]{2,1,0:T(8,128)} %get-tuple-element.12), custom_call_target="InvertDiagBlocksLowerTriangular" | custom-call | tf_op jit(solution)/shard_map/jit(_cho_solve)/triangular_solve | solution.py:29
  303.7 5.7 %all-to-all-start.1 = ((bf16[64,8,1024]{2,0,1:T(8,128)(2,1)}), bf16[64,8,1024]{2,0,1:T(8,128)(2,1)S(1)}, u32[]{:S(2)}, u32[]{:S(2)}) async-start(bf16[64,8,1024]{2,0,1:T(8,128)(2,1)} %copy.48), calls=%async_computation.1 | async-start | bytes 2097152 | tf_op jit(solution)/shard_map/all_to_all | solution.py:39
  314.6 20.2 %all-to-all-done.1 = bf16[64,8,1024]{2,0,1:T(8,128)(2,1)S(1)} async-done(((bf16[64,8,1024]{2,0,1:T(8,128)(2,1)}), bf16[64,8,1024]{2,0,1:T(8,128)(2,1)S(1)}, u32[]{:S(2)}, u32[]{:S(2)}) %all-to-all-start.1) | async-done | bytes 1048608 | tf_op jit(solution)/shard_map/all_to_all | solution.py:39
  335.3 3.7 add_convert_fusion
  338.9 29.1 %all_to_all.79 = bf16[8,64,1024]{2,1,0:T(8,128)(2,1)S(1)} all-to-all(bf16[8,64,1024]{2,1,0:T(8,128)(2,1)S(1)} %bitcast.106), channel_id=1, replica_groups=mesh['member'=8,'region'=4] {'member'}, dimensions={0} | all-to-all | bytes 2097152 | tf_op jit(solution)/shard_map/all_to_all | solution.py:76
  369.1 16.9 %all_to_all.80 = bf16[4,16,8192]{2,1,0:T(8,128)(2,1)S(1)} all-to-all(bf16[4,16,8192]{2,1,0:T(8,128)(2,1)S(1)} %all_to_all.70), channel_id=1, replica_groups=mesh['member'=8,'region'=4] {'region'}, dimensions={0} | all-to-all | bytes 2097152 | tf_op jit(solution)/shard_map/all_to_all | solution.py:75
  (115 shorter events, 47.4 us)
Async XLA Ops:
  34.4 16.7 %copy-start.5 = (u32[32]{0:T(128)S(1)}, u32[32]{0:T(128)}, u32[]{:S(2)}) copy-start(u32[32]{0:T(128)} %constant.210) | copy-start | bytes 388
  34.5 18.1 %copy-start.3 = (f32[1,1,16]{2,1,0:T(1,128)S(1)}, f32[1,1,16]{2,1,0:T(1,128)}, u32[]{:S(2)}) copy-start(f32[1,1,16]{2,1,0:T(1,128)} %param.7) | copy-start | bytes 196
  34.5 18.2 %copy-start.4 = (f32[1,1,16]{2,1,0:T(1,128)S(1)}, f32[1,1,16]{2,1,0:T(1,128)}, u32[]{:S(2)}) copy-start(f32[1,1,16]{2,1,0:T(1,128)} %param.6) | copy-start | bytes 196
  41.5 69.9 %copy-start.1 = (bf16[16,32768]{1,0:T(8,128)(2,1)S(1)}, bf16[16,32768]{1,0:T(8,128)(2,1)}, u32[]{:S(2)}) copy-start(bf16[16,32768]{1,0:T(8,128)(2,1)} %param.4) | copy-start | bytes 3145732
  47.9 22.0 %all-to-all-start.2 = ((bf16[16,4,128]{2,0,1:T(8,128)(2,1)}), bf16[16,4,128]{2,0,1:T(8,128)(2,1)S(1)}, u32[]{:S(2)}, u32[]{:S(2)}) async-start(bf16[16,4,128]{2,0,1:T(8,128)(2,1)} %broadcast_select_fusion), calls=%async_computation.2 | async-start | bytes 32768 | tf_op jit(solution)/shard_map/all_to_all | solution.py:54
  51.1 103.1 %all-reduce.7.cloned.1.call-start = ((), (), s32[]{:S(2)}) async-start(), calls=%async_computation.5 | async-start | bytes 2097152 | tf_op jit(solution)/shard_map/psum | solution.py:68
  112.5 187.8 %all-to-all-start = ((bf16[16,4,8192]{2,0,1:T(8,128)(2,1)}), bf16[16,4,8192]{2,0,1:T(8,128)(2,1)}, u32[]{:S(2)}, u32[]{:S(2)}) async-start(bf16[16,4,8192]{2,0,1:T(8,128)(2,1)} %bitcast.95), calls=%async_computation | async-start | bytes 2097152 | tf_op jit(solution)/shard_map/all_to_all | solution.py:40
  154.2 2.9 copy-start
  158.6 34.3 %copy-start.2 = (f32[512,512]{1,0:T(8,128)}, f32[512,512]{1,0:T(8,128)S(1)}, u32[]{:S(2)}) copy-start(f32[512,512]{1,0:T(8,128)S(1)} %fusion.4) | copy-start | bytes 3145732
  303.7 31.1 %all-to-all-start.1 = ((bf16[64,8,1024]{2,0,1:T(8,128)(2,1)}), bf16[64,8,1024]{2,0,1:T(8,128)(2,1)S(1)}, u32[]{:S(2)}, u32[]{:S(2)}) async-start(bf16[64,8,1024]{2,0,1:T(8,128)(2,1)} %copy.48), calls=%async_computation.1 | async-start | bytes 2097152 | tf_op jit(solution)/shard_map/all_to_all | solution.py:39
Sparse Core Ops, SparseCore 0:
  111.6 42.6 all-reduce.6
where the time goes:
time: 399 us; the launch traced here: 394 us
  blocking collectives  150 us (38%)
  other arithmetic  125 us (31%)
  waiting for transfers between devices  34.9 us (9%)
  local copies, waits for them, and re-layouts  33.3 us (8%)
  matrix products  19.1 us (5%)
  between operations  18.6 us (5%)
  starting transfers between devices  13.2 us (3%)
    another operation x14, other arithmetic, mixing_matrix(): factor = jnp.linalg.cholesky(system)  79 us
    another operation x3, other arithmetic, mixing_matrix(): solved = jax.scipy.linalg.cho_solve((factor, True), right_side)  40.3 us
    all_gather x1, blocking collectives, local(): obs_rows = lax.all_gather(local_rows, 'member', axis=0, tiled=True)  30.5 us
    all_to_all x1, blocking collectives, local(): lax.all_to_all(updated, 'member', split_axis=0, concat_axis=1, tiled=True)  29.1 us
    all_gather x1, blocking collectives, local(): region_offsets = lax.all_gather(obs_offset, 'member', axis=1, tiled=True)  22.5 us
    psum x1, blocking collectives, local(): products, column = lax.psum((products, column), 'region')  22.4 us
    all_to_all x1, waiting for transfers between devices, local(): lax.all_to_all(lax.all_to_all(ensemble, 'region', split_axis=1, concat_ax...  20.2 us
    all_gather x1, blocking collectives, local(): lax.all_gather(variance, 'member', axis=0, tiled=True)  17.1 us
  transfers between devices with their start and end apart: 4, of which 2 were waited for; matrix products, arithmetic and copies ran while one was open for 38% of the time, Pallas kernels for 0%

commit v1 on v0

--- a/solution.py
+++ b/solution.py
@@ -1,7 +1,27 @@
+import functools
 import jax
 import jax.numpy as jnp
 from jax import lax
 from jax.sharding import PartitionSpec as P
+
+
+def panels_draft(my_data, mesh_dim, row_dim):
+    full_n = lax.psum(1, mesh_dim)
+    val = sorted(((no, (no + 1) % full_n) for no in range(full_n)))
+    y_new = my_data
+    series = [y_new]
+    i = 1
+    while i < full_n:
+        y_new = lax.ppermute(y_new, mesh_dim, val)
+        series.insert(0, y_new)
+        i = i + 1
+    plain = jnp.concatenate(series, axis=row_dim)
+    all_values = lax.axis_index(mesh_dim)
+    h_now = all_values + 1
+    return jnp.roll(plain, h_now * my_data.shape[row_dim], axis=row_dim)
+
+
+outputs_map = functools.partial(panels_draft, mesh_dim="member", row_dim=0)
 
 
 def observation_terms(picked, values, variance, ensemble_size):
@@ -53,7 +73,7 @@
     own_rows = jnp.take(ensemble, link_index, axis=1).reshape(own_count, regions, -1)
     local_rows = lax.all_to_all(own_rows, "region", split_axis=1, concat_axis=0, tiled=True)
     local_rows = local_rows.reshape(own_count * regions, -1)
-    obs_rows = lax.all_gather(local_rows, "member", axis=0, tiled=True)
+    obs_rows = outputs_map(local_rows)
     region_values, region_variance = (
         lax.all_gather(values, "member", axis=0, tiled=True),
         lax.all_gather(variance, "member", axis=0, tiled=True),

time: 399 us -> 410 us (1.028)
  waiting for transfers between devices: 34.9 us -> 70.9 us
  blocking collectives: 150 us -> 128 us
    ppermute x0 -> x7, waiting for transfers between devices: none -> 37.3 us  [panels_draft(): y_new = lax.ppermute(y_new, mesh_dim, val)]
    all_gather x1 -> x0, blocking collectives: 30.5 us -> none  [local(): obs_rows = lax.all_gather(local_rows, 'member', axis=0, tiled=True)]
    all_to_all x0 -> x1, blocking collectives: none -> 6.42 us  [local(): lax.all_to_all(own_rows, 'region', split_axis=1, concat_axis=0, tiled=True)]
    all_gather x1, blocking collectives: 17.1 us -> 21.8 us  [local(): lax.all_gather(variance, 'member', axis=0, tiled=True)]
    unnamed x19 -> x34, local copies, waits for them, and re-layouts: 9.77 us -> 9.83 us
  transfers between devices with their start and end apart: 4 -> 10, of which waited for: 2 -> 8; matrix products, arithmetic and copies ran while one was open for 38% -> 37% of each run, Pallas kernels for 0% -> 0%
where the time goes in v1:
time: 410 us; the launch traced here: 405 us
  blocking collectives  128 us (31%)
  other arithmetic  124 us (30%)
  waiting for transfers between devices  70.9 us (17%)
  local copies, waits for them, and re-layouts  33.4 us (8%)
  matrix products  19.1 us (5%)
  between operations  18.6 us (5%)
  starting transfers between devices  9.97 us (2%)
    another operation x14, other arithmetic, mixing_matrix(): factor = jnp.linalg.cholesky(system)  79 us
    another operation x3, other arithmetic, mixing_matrix(): solved = jax.scipy.linalg.cho_solve((factor, True), right_side)  40.3 us
    ppermute x7, waiting for transfers between devices, panels_draft(): y_new = lax.ppermute(y_new, mesh_dim, val)  37.3 us
    all_to_all x1, blocking collectives, local(): lax.all_to_all(updated, 'member', split_axis=0, concat_axis=1, tiled=True)  29.1 us
    all_gather x1, blocking collectives, local(): region_offsets = lax.all_gather(obs_offset, 'member', axis=1, tiled=True)  22.5 us
    all_gather x1, blocking collectives, local(): lax.all_gather(variance, 'member', axis=0, tiled=True)  21.8 us
    all_to_all x1, waiting for transfers between devices, local(): lax.all_to_all(lax.all_to_all(ensemble, 'region', split_axis=1, concat_ax...  20.2 us
    psum x1, blocking collectives, local(): products, column = lax.psum((products, column), 'region')  20.1 us
  transfers between devices with their start and end apart: 10, of which 8 were waited for; matrix products, arithmetic and copies ran while one was open for 37% of the time, Pallas kernels for 0%

profile of v1, /device:TPU:0, one launch (start us, length us, event | category | flops | bytes accessed | tf_op | source)
XLA Modules:
  0.0 404.7 jit_solution(14795665674492368618)
XLA Ops:
  6.5 22.5 %all_gather.13 = s32[1,8,16]{2,0,1:T(1,128)S(1)} all-gather(s32[1,1,16]{2,0,1:T(1,128)} %bitcast.114), channel_id=1, replica_groups=mesh['member'=8,'region'=4] {'member'}, dimensions={1}, use_global_device_ids=true | all-gather | bytes 576 | tf_op jit(solution)/shard_map/all_gather | solution.py:68
  34.5 7.1 %copy.51 = bf16[16,32768]{0,1:T(8,128)(2,1)} copy(bf16[16,32768]{1,0:T(8,128)(2,1)} %param.4) | data formatting | bytes 2097152 | tf_op args[0]
  47.3 6.4 %all_to_all.79 = bf16[16,4,128]{2,0,1:T(8,128)(2,1)S(1)} all-to-all(bf16[16,4,128]{2,0,1:T(8,128)(2,1)S(1)} %broadcast_select_fusion), channel_id=1, replica_groups=mesh['member'=8,'region'=4] {'region'}, dimensions={1} | all-to-all | bytes 32768 | tf_op jit(solution)/shard_map/all_to_all | solution.py:74
  53.7 6.4 %collective-permute-done = bf16[64,128]{1,0:T(8,128)(2,1)S(1)} collective-permute-done((bf16[64,128]{1,0:T(8,128)(2,1)S(1)}, bf16[64,128]{1,0:T(8,128)(2,1)S(1)}, u32[]{:S(2)}, u32[]{:S(2)}) %collective-permute-start) | collective-permute-done | bytes 16416 | tf_op jit(solution)/shard_map/ppermute | solution.py:15
  60.1 6.4 %collective-permute-done.1 = bf16[64,128]{1,0:T(8,128)(2,1)S(1)} collective-permute-done((bf16[64,128]{1,0:T(8,128)(2,1)S(1)}, bf16[64,128]{1,0:T(8,128)(2,1)S(1)}, u32[]{:S(2)}, u32[]{:S(2)}) %collective-permute-start.1) | collective-permute-done | bytes 16416 | tf_op jit(solution)/shard_map/ppermute | solution.py:15
  66.6 6.4 %collective-permute-done.2 = bf16[64,128]{1,0:T(8,128)(2,1)S(1)} collective-permute-done((bf16[64,128]{1,0:T(8,128)(2,1)S(1)}, bf16[64,128]{1,0:T(8,128)(2,1)S(1)}, u32[]{:S(2)}, u32[]{:S(2)}) %collective-permute-start.2) | collective-permute-done | bytes 16416 | tf_op jit(solution)/shard_map/ppermute | solution.py:15
  73.0 6.4 %collective-permute-done.3 = bf16[64,128]{1,0:T(8,128)(2,1)S(1)} collective-permute-done((bf16[64,128]{1,0:T(8,128)(2,1)S(1)}, bf16[64,128]{1,0:T(8,128)(2,1)S(1)}, u32[]{:S(2)}, u32[]{:S(2)}) %collective-permute-start.3) | collective-permute-done | bytes 16416 | tf_op jit(solution)/shard_map/ppermute | solution.py:15
  86.0 6.3 %collective-permute-done.5 = bf16[64,128]{1,0:T(8,128)(2,1)S(1)} collective-permute-done((bf16[64,128]{1,0:T(8,128)(2,1)S(1)}, bf16[64,128]{1,0:T(8,128)(2,1)S(1)}, u32[]{:S(2)}, u32[]{:S(2)}) %collective-permute-start.5) | collective-permute-done | bytes 16416 | tf_op jit(solution)/shard_map/ppermute | solution.py:15
  92.4 21.8 %all-reduce.3 = (f32[128]{0:T(128)S(1)}, f32[128]{0:T(128)S(1)}) all-reduce(f32[128]{0:T(128)S(1)} %bitcast_dynamic-update-slice_fusion.1, f32[128]{0:T(128)S(1)} %bitcast_dynamic-update-slice_fusion.2), channel_id=3, replica_groups=mesh['member'=8,'region'=4] {'member'}, use_global_device_ids=true, to_apply=%add.2 | all-reduce | flops 256 | bytes 2048 | tf_op jit(solution)/shard_map/all_gather | solution.py:79
  115.9 6.4 %all-reduce.4 = (f32[]{:T(128)}, f32[]{:T(128)}) all-reduce(f32[]{:T(128)} %get-tuple-element.54, f32[]{:T(128)} %get-tuple-element.51), channel_id=1, replica_groups=mesh['member'=8,'region'=4] {'region'}, use_global_device_ids=true, to_apply=%region_3.4 | all-reduce | flops 2 | bytes 16 | tf_op jit(solution)/shard_map/psum | solution.py:85
  131.2 20.1 %psum.31 = f32[512,1]{0,1:T(1,128)S(1)} all-reduce(f32[512,1]{0,1:T(1,128)S(1)} %convolution_bitcast_fusion), channel_id=1, replica_groups=mesh['member'=8,'region'=4] {'region'}, use_global_device_ids=true, to_apply=%region_16.17 | all-reduce | flops 512 | bytes 4096 | tf_op jit(solution)/shard_map/psum | solution.py:88
  151.4 13.5 %all-reduce.7.cloned.1.call-done = f32[512,512]{0,1:T(8,128)} async-done(((f32[512,512]{0,1:T(8,128)}), f32[512,512]{0,1:T(8,128)}) %all-reduce.7.cloned.1.call-update) | async-done | bytes 1048592 | tf_op jit(solution)/shard_map/psum | solution.py:88
  169.3 11.7 %cholesky.103 = f32[128,128]{1,0:T(8,128)S(1)} custom-call(f32[128,128]{1,0:T(8,128)S(1)} %cholesky.263), custom_call_target="Cholesky" | custom-call | tf_op jit(solution)/shard_map/jit(cholesky)/cholesky | solution.py:47
  181.0 9.8 %custom-call.34 = f32[1,128,128]{1,2,0:T(8,128)S(1)} custom-call(f32[1,128,128]{2,1,0:T(8,128)S(1)} %get-tuple-element.50), custom_call_target="InvertDiagBlocksLowerTriangular" | custom-call | tf_op jit(solution)/shard_map/jit(cholesky)/cholesky | solution.py:47
  191.5 11.7 %cholesky.215 = f32[128,128]{1,0:T(8,128)S(1)} custom-call(f32[128,128]{1,0:T(8,128)S(1)} %cholesky.267), custom_call_target="Cholesky" | custom-call | tf_op jit(solution)/shard_map/jit(cholesky)/cholesky | solution.py:47
  203.6 10.0 %custom-call.35 = f32[1,128,128]{1,2,0:T(8,128)S(1)} custom-call(f32[1,128,128]{2,1,0:T(8,128)S(1)} %get-tuple-element.48), custom_call_target="InvertDiagBlocksLowerTriangular" | custom-call | tf_op jit(solution)/shard_map/jit(cholesky)/cholesky | solution.py:47
  215.6 11.7 %cholesky.236 = f32[128,128]{1,0:T(8,128)S(1)} custom-call(f32[128,128]{1,0:T(8,128)S(1)} %cholesky.272), custom_call_target="Cholesky" | custom-call | tf_op jit(solution)/shard_map/jit(cholesky)/cholesky | solution.py:47
  227.5 9.8 %custom-call.36 = f32[1,128,128]{1,2,0:T(8,128)S(1)} custom-call(f32[1,128,128]{2,1,0:T(8,128)S(1)} %get-tuple-element.46), custom_call_target="InvertDiagBlocksLowerTriangular" | custom-call | tf_op jit(solution)/shard_map/jit(cholesky)/cholesky | solution.py:47
  238.9 12.1 %cholesky.253 = f32[128,128]{1,0:T(8,128)S(1)} custom-call(f32[128,128]{1,0:T(8,128)S(1)} %convolution_subtract_fusion.8), custom_call_target="Cholesky" | custom-call | tf_op jit(solution)/shard_map/jit(cholesky)/cholesky | solution.py:47
  255.9 11.0 %while.1 = (s32[]{:T(128)}, f32[512,512]{0,1:T(8,128)S(1)}, s32[4,2]{0,1:T(2,128)S(1)}, f32[4,128,128]{2,1,0:T(8,128)}, s32[]{:T(128)}) while((s32[]{:T(128)}, f32[512,512]{0,1:T(8,128)S(1)}, s32[4,2]{0,1:T(2,128)S(1)}, f32[4,128,128]{2,1,0:T(8,128)}, s32[]{:T(128)}) %tuple.30), condition=%wide.while_cond, body=%wide.while_body.sunk | while | flops 2 | bytes 393829 | solution.py:49
  266.8 40.1 %custom-call.37 = f32[4,128,128]{1,2,0:T(8,128)S(1)} custom-call(f32[4,128,128]{2,1,0:T(8,128)} %get-tuple-element.12), custom_call_target="InvertDiagBlocksLowerTriangular" | custom-call | tf_op jit(solution)/shard_map/jit(_cho_solve)/triangular_solve | solution.py:49
  325.2 20.2 %all-to-all-done.1 = bf16[64,8,1024]{2,0,1:T(8,128)(2,1)S(1)} async-done(((bf16[64,8,1024]{2,0,1:T(8,128)(2,1)}), bf16[64,8,1024]{2,0,1:T(8,128)(2,1)S(1)}, u32[]{:S(2)}, u32[]{:S(2)}) %all-to-all-start.1) | async-done | bytes 1048608 | tf_op jit(solution)/shard_map/all_to_all | solution.py:59
  349.6 29.1 %all_to_all.80 = bf16[8,64,1024]{2,1,0:T(8,128)(2,1)S(1)} all-to-all(bf16[8,64,1024]{2,1,0:T(8,128)(2,1)S(1)} %bitcast.106), channel_id=1, replica_groups=mesh['member'=8,'region'=4] {'member'}, dimensions={0} | all-to-all | bytes 2097152 | tf_op jit(solution)/shard_map/all_to_all | solution.py:96
  379.8 16.9 %all_to_all.81 = bf16[4,16,8192]{2,1,0:T(8,128)(2,1)S(1)} all-to-all(bf16[4,16,8192]{2,1,0:T(8,128)(2,1)S(1)} %all_to_all.70), channel_id=1, replica_groups=mesh['member'=8,'region'=4] {'region'}, dimensions={0} | all-to-all | bytes 2097152 | tf_op jit(solution)/shard_map/all_to_all | solution.py:95
  (143 shorter events, 73.2 us)
Async XLA Ops:
  6.5 158.3 %all-reduce.7.cloned.1.call-start = ((), (), s32[]{:S(2)}) async-start(), calls=%async_computation.5 | async-start | bytes 2097152 | tf_op jit(solution)/shard_map/psum | solution.py:88
  34.4 45.0 %copy-start.5 = (u32[32]{0:T(128)S(1)}, u32[32]{0:T(128)}, u32[]{:S(2)}) copy-start(u32[32]{0:T(128)} %constant.241) | copy-start | bytes 388
  34.5 51.4 %copy-start.3 = (f32[1,1,16]{2,1,0:T(1,128)S(1)}, f32[1,1,16]{2,1,0:T(1,128)}, u32[]{:S(2)}) copy-start(f32[1,1,16]{2,1,0:T(1,128)} %param.7) | copy-start | bytes 196
  34.5 57.8 %copy-start.4 = (f32[1,1,16]{2,1,0:T(1,128)S(1)}, f32[1,1,16]{2,1,0:T(1,128)}, u32[]{:S(2)}) copy-start(f32[1,1,16]{2,1,0:T(1,128)} %param.6) | copy-start | bytes 196
  41.5 84.1 %copy-start.1 = (bf16[16,32768]{1,0:T(8,128)(2,1)S(1)}, bf16[16,32768]{1,0:T(8,128)(2,1)}, u32[]{:S(2)}) copy-start(bf16[16,32768]{1,0:T(8,128)(2,1)} %param.4) | copy-start | bytes 3145732
  53.7 6.4 %collective-permute-start = (bf16[64,128]{1,0:T(8,128)(2,1)S(1)}, bf16[64,128]{1,0:T(8,128)(2,1)S(1)}, u32[]{:S(2)}, u32[]{:S(2)}) collective-permute-start(bf16[64,128]{1,0:T(8,128)(2,1)S(1)} %bitcast.108), channel_id=1, source_target_pairs={{0,4},{4,8},{8,12},{12,16},{16,20},{20,24},{24,28},{28,0},{1,5},{5... | collective-permute-start | bytes 49160 | tf_op jit(solution)/shard_map/ppermute | solution.py:15
  60.1 6.4 %collective-permute-start.1 = (bf16[64,128]{1,0:T(8,128)(2,1)S(1)}, bf16[64,128]{1,0:T(8,128)(2,1)S(1)}, u32[]{:S(2)}, u32[]{:S(2)}) collective-permute-start(bf16[64,128]{1,0:T(8,128)(2,1)S(1)} %collective-permute-done), channel_id=1, source_target_pairs={{0,4},{4,8},{8,12},{12,16},{16,20},{20,24},{24,28},{28,0},{1,5},{5... | collective-permute-start | bytes 49160 | tf_op jit(solution)/shard_map/ppermute | solution.py:15
  66.6 6.4 %collective-permute-start.2 = (bf16[64,128]{1,0:T(8,128)(2,1)S(1)}, bf16[64,128]{1,0:T(8,128)(2,1)S(1)}, u32[]{:S(2)}, u32[]{:S(2)}) collective-permute-start(bf16[64,128]{1,0:T(8,128)(2,1)S(1)} %collective-permute-done.1), channel_id=1, source_target_pairs={{0,4},{4,8},{8,12},{12,16},{16,20},{20,24},{24,28},{28,0},{1,5},{5... | collective-permute-start | bytes 49160 | tf_op jit(solution)/shard_map/ppermute | solution.py:15
  73.0 6.4 %collective-permute-start.3 = (bf16[64,128]{1,0:T(8,128)(2,1)S(1)}, bf16[64,128]{1,0:T(8,128)(2,1)S(1)}, u32[]{:S(2)}, u32[]{:S(2)}) collective-permute-start(bf16[64,128]{1,0:T(8,128)(2,1)S(1)} %collective-permute-done.2), channel_id=1, source_target_pairs={{0,4},{4,8},{8,12},{12,16},{16,20},{20,24},{24,28},{28,0},{1,5},{5... | collective-permute-start | bytes 49160 | tf_op jit(solution)/shard_map/ppermute | solution.py:15
  79.4 6.4 %collective-permute-start.4 = (bf16[64,128]{1,0:T(8,128)(2,1)S(1)}, bf16[64,128]{1,0:T(8,128)(2,1)S(1)}, u32[]{:S(2)}, u32[]{:S(2)}) collective-permute-start(bf16[64,128]{1,0:T(8,128)(2,1)S(1)} %collective-permute-done.3), channel_id=1, source_target_pairs={{0,4},{4,8},{8,12},{12,16},{16,20},{20,24},{24,28},{28,0},{1,5},{5... | collective-permute-start | bytes 49160 | tf_op jit(solution)/shard_map/ppermute | solution.py:15
  85.9 6.4 %collective-permute-start.5 = (bf16[64,128]{1,0:T(8,128)(2,1)S(1)}, bf16[64,128]{1,0:T(8,128)(2,1)S(1)}, u32[]{:S(2)}, u32[]{:S(2)}) collective-permute-start(bf16[64,128]{1,0:T(8,128)(2,1)S(1)} %collective-permute-done.4), channel_id=1, source_target_pairs={{0,4},{4,8},{8,12},{12,16},{16,20},{20,24},{24,28},{28,0},{1,5},{5... | collective-permute-start | bytes 49160 | tf_op jit(solution)/shard_map/ppermute | solution.py:15
  92.3 21.9 %collective-permute-start.6 = (bf16[64,128]{1,0:T(8,128)(2,1)S(1)}, bf16[64,128]{1,0:T(8,128)(2,1)S(1)}, u32[]{:S(2)}, u32[]{:S(2)}) collective-permute-start(bf16[64,128]{1,0:T(8,128)(2,1)S(1)} %collective-permute-done.5), channel_id=1, source_target_pairs={{0,4},{4,8},{8,12},{12,16},{16,20},{20,24},{24,28},{28,0},{1,5},{5... | collective-permute-start | bytes 49160 | tf_op jit(solution)/shard_map/ppermute | solution.py:15
  126.6 184.3 %all-to-all-start = ((bf16[16,4,8192]{2,0,1:T(8,128)(2,1)}), bf16[16,4,8192]{2,0,1:T(8,128)(2,1)}, u32[]{:S(2)}, u32[]{:S(2)}) async-start(bf16[16,4,8192]{2,0,1:T(8,128)(2,1)} %bitcast.95), calls=%async_computation | async-start | bytes 2097152 | tf_op jit(solution)/shard_map/all_to_all | solution.py:60
  164.8 2.9 copy-start
  169.2 34.3 %copy-start.2 = (f32[512,512]{1,0:T(8,128)}, f32[512,512]{1,0:T(8,128)S(1)}, u32[]{:S(2)}) copy-start(f32[512,512]{1,0:T(8,128)S(1)} %fusion.4) | copy-start | bytes 3145732
  314.3 31.1 %all-to-all-start.1 = ((bf16[64,8,1024]{2,0,1:T(8,128)(2,1)}), bf16[64,8,1024]{2,0,1:T(8,128)(2,1)S(1)}, u32[]{:S(2)}, u32[]{:S(2)}) async-start(bf16[64,8,1024]{2,0,1:T(8,128)(2,1)} %copy.48), calls=%async_computation.1 | async-start | bytes 2097152 | tf_op jit(solution)/shard_map/all_to_all | solution.py:59
Sparse Core Ops, SparseCore 0:
  125.7 39.0 all-reduce.6
